TPU v7x, 32 devices: a whole 2x2x4 slice. The times are simulated.
32 devices in a mesh: dp: 8 (over z, x), patch: 4 (over y, core).
Axes of the slice: x: 2, y: 2, z: 4, core: 2. Of those that a mesh axis runs over, the one named last changes fastest.
Arguments:
- query_rows: bfloat16 [8, 512, 576], P('dp', 'patch'), may hold values from -6 to 6
- key_rows: bfloat16 [8, 512, 576], P('dp', 'patch'), may hold values from -6 to 6
- value_rows: bfloat16 [8, 512, 576], P('dp', 'patch'), may hold values from -6 to 6
- out_weight: bfloat16 [576, 1152], replicated, may hold values from -0.25 to 0.25
- target: bfloat16 [8, 512, 1152], P('dp', 'patch'), may hold values from -6 to 6
- lengths: int32 [8], P('dp'), may hold values from 64 to 512
- segments: int32 [8, 512], P('dp', 'patch'), may hold values from 0 to 7, never falling along the last dimension, each value on 1 to 256 neighbouring positions
Outputs:
- query_grad: float32 [8, 512, 576], P('dp', 'patch')
- key_grad: float32 [8, 512, 576], P('dp', 'patch')
- value_grad: float32 [8, 512, 576], P('dp', 'patch')
- weight_grad: float32 [576, 1152], P('patch', 'dp')
- loss: float32 [], replicated
All inputs are finite; a program needn't handle non-finite values.
Results may differ from a plain program's by a relative error of at most 0.024.
Values may be sent and summed in bfloat16 or wider, within the bound.
A program may use at most 64 MiB of HBM per device.

v0:
```python
import math

import jax
import jax.numpy as jnp
from jax import lax
from jax.sharding import PartitionSpec as P

WIDTH = 1152
HEADS = 8
HEAD_DIM = 72
FEAT = 576


NEG_LARGE = -1e30


def head_view(rows):
    return rows.reshape(rows.shape[0], HEADS, HEAD_DIM)


def pair_mask(query_group, key_group):
    return (query_group[:, None] == key_group[None, :])[None, :, :]


def forward_block(running, query_heads, own_group, group_all, pieces, first_row):
    run_max, run_denom, run_accum = running
    score_scale = 1.0 / math.sqrt(HEAD_DIM)
    key_heads = head_view(pieces[0][0])
    value_heads = head_view(pieces[1][0])
    piece_rows = key_heads.shape[0]
    allowed = pair_mask(own_group, lax.dynamic_slice_in_dim(group_all, first_row, piece_rows, 0))
    scores = (
        jnp.einsum("qhe,khe->hqk", query_heads, key_heads, preferred_element_type=jnp.float32)
        * score_scale
    )
    masked = jnp.where(allowed, scores, NEG_LARGE)
    new_max = jnp.maximum(run_max, jnp.max(masked, axis=2))
    probs = jnp.where(allowed, jnp.exp(masked - new_max[:, :, None]), 0.0)
    shrink = jnp.exp(run_max - new_max)
    run_denom = run_denom * shrink + jnp.sum(probs, axis=2)
    added = jnp.einsum(
        "hqk,khe->qhe", probs.astype(jnp.bfloat16), value_heads, preferred_element_type=jnp.float32
    )
    run_accum = run_accum * shrink.T[:, :, None] + added
    return (new_max, run_denom, run_accum)


def query_grad_block(
    running, query_heads, grad_heads, log_norm, delta, own_group, group_all, pieces, first_row
):
    score_scale = 1.0 / math.sqrt(HEAD_DIM)
    key_heads = head_view(pieces[0][0])
    value_heads = head_view(pieces[1][0])
    piece_rows = key_heads.shape[0]
    allowed = pair_mask(own_group, lax.dynamic_slice_in_dim(group_all, first_row, piece_rows, 0))
    scores = (
        jnp.einsum("qhe,khe->hqk", query_heads, key_heads, preferred_element_type=jnp.float32)
        * score_scale
    )
    masked = jnp.where(allowed, scores, NEG_LARGE)
    probs = jnp.where(allowed, jnp.exp(masked - log_norm[:, :, None]), 0.0)
    dprobs = jnp.einsum("qhe,khe->hqk", grad_heads, value_heads, preferred_element_type=jnp.float32)
    dscores = (probs * (dprobs - delta[:, :, None])).astype(jnp.bfloat16)
    return (
        running
        + jnp.einsum("hqk,khe->qhe", dscores, key_heads, preferred_element_type=jnp.float32)
        * score_scale
    )


def key_grad_block(own_keys, own_values, own_group, group_all, log_all, delta_all, pieces):
    score_scale = 1.0 / math.sqrt(HEAD_DIM)
    query_heads = head_view(pieces[0][0])
    grad_heads = head_view(pieces[1][0])
    allowed = pair_mask(group_all, own_group)
    scores = (
        jnp.einsum("qhe,khe->hqk", query_heads, own_keys, preferred_element_type=jnp.float32)
        * score_scale
    )
    masked = jnp.where(allowed, scores, NEG_LARGE)
    probs = jnp.where(allowed, jnp.exp(masked - log_all[:, :, None]), 0.0)
    grad_values = jnp.einsum(
        "hqk,qhe->khe", probs.astype(jnp.bfloat16), grad_heads, preferred_element_type=jnp.float32
    )
    dprobs = jnp.einsum("qhe,khe->hqk", grad_heads, own_values, preferred_element_type=jnp.float32)
    dscores = (probs * (dprobs - delta_all[:, :, None])).astype(jnp.bfloat16)
    grad_keys = (
        jnp.einsum("hqk,qhe->khe", dscores, query_heads, preferred_element_type=jnp.float32)
        * score_scale
    )
    return (grad_keys, grad_values)


def sweep_blocks(step_fn, running, key_all, value_all):
    total_keys = key_all.shape[1]
    block_rows = math.gcd(512, total_keys)

    def advance(block_index, current):
        first_row = block_index * block_rows
        pieces = (
            lax.dynamic_slice_in_dim(key_all, first_row, block_rows, 1),
            lax.dynamic_slice_in_dim(value_all, first_row, block_rows, 1),
        )
        return step_fn(current, pieces, first_row)

    return lax.fori_loop(0, total_keys // block_rows, advance, running)


def local(query_rows, key_rows, value_rows, out_weight, target, lengths, segments):
    own_rows = query_rows.shape[1]
    members = lax.axis_size("patch")
    groups = lax.axis_size("dp")
    total_rows = own_rows * members
    length = lengths[0]
    count = lax.psum(length.astype(jnp.float32), "dp")
    offset = lax.axis_index("patch") * own_rows
    own_live = offset + lax.iota(jnp.int32, own_rows) < length
    segment_all = lax.all_gather(segments, "patch", axis=1, tiled=True)
    group_all = jnp.where(lax.iota(jnp.int32, total_rows) < length, segment_all[0], -1)
    own_group = lax.dynamic_slice_in_dim(group_all, offset, own_rows, 0)
    query_heads = head_view(query_rows[0])
    starting = (
        jnp.full((HEADS, own_rows), NEG_LARGE, jnp.float32),
        jnp.zeros((HEADS, own_rows), jnp.float32),
        jnp.zeros((own_rows, HEADS, HEAD_DIM), jnp.float32),
    )

    def forward_step(running, pieces, first_row):
        return forward_block(running, query_heads, own_group, group_all, pieces, first_row)

    key_all, value_all = (
        lax.all_gather(key_rows, "patch", axis=1, tiled=True),
        lax.all_gather(value_rows, "patch", axis=1, tiled=True),
    )
    forward_state = sweep_blocks(forward_step, starting, key_all, value_all)
    run_max, run_denom, run_accum = forward_state
    log_norm = run_max + jnp.log(run_denom)
    attn = (run_accum / run_denom.T[:, :, None]).reshape(own_rows, FEAT).astype(jnp.bfloat16)
    output = jnp.dot(attn, out_weight, preferred_element_type=jnp.float32)
    error = jnp.where(own_live[:, None], output - target[0].astype(jnp.float32), 0.0)
    loss_part = jnp.sum(error * error)
    grad_out = (2.0 * error).astype(jnp.bfloat16)
    weight_part = jnp.einsum("tf,td->fd", attn, grad_out, preferred_element_type=jnp.float32)
    grad_attn = jnp.einsum(
        "td,fd->tf", grad_out, out_weight, preferred_element_type=jnp.float32
    ).astype(jnp.bfloat16)
    delta = jnp.sum(
        (grad_attn.astype(jnp.float32) * attn.astype(jnp.float32)).reshape(
            own_rows, HEADS, HEAD_DIM
        ),
        axis=2,
    ).T
    grad_heads = head_view(grad_attn)

    def query_step(running, pieces, first_row):
        return query_grad_block(
            running,
            query_heads,
            grad_heads,
            log_norm,
            delta,
            own_group,
            group_all,
            pieces,
            first_row,
        )

    zero_heads = jnp.zeros((own_rows, HEADS, HEAD_DIM), jnp.float32)
    query_raw = sweep_blocks(query_step, zero_heads, key_all, value_all)
    log_all, delta_all = (
        lax.all_gather(log_norm, "patch", axis=1, tiled=True),
        lax.all_gather(delta, "patch", axis=1, tiled=True),
    )
    own_keys = head_view(key_rows[0])
    own_values = head_view(value_rows[0])
    key_raw, value_raw = key_grad_block(
        own_keys,
        own_values,
        own_group,
        group_all,
        log_all,
        delta_all,
        (
            lax.all_gather(query_rows, "patch", axis=1, tiled=True),
            lax.all_gather(grad_attn[None], "patch", axis=1, tiled=True),
        ),
    )
    loss_total = lax.psum(loss_part, ("dp", "patch"))
    row_share = lax.psum_scatter(
        weight_part.astype(jnp.bfloat16), "patch", scatter_dimension=0, tiled=True
    )
    weight_share = lax.psum_scatter(row_share, "dp", scatter_dimension=1, tiled=True).astype(
        jnp.float32
    )
    ratio = jnp.float32(groups * total_rows) / count
    query_grad = (ratio * query_raw).reshape(1, own_rows, FEAT)
    key_grad = (ratio * key_raw).reshape(1, own_rows, FEAT)
    value_grad = (ratio * value_raw).reshape(1, own_rows, FEAT)
    weight_grad = weight_share * (ratio / total_rows)
    loss = loss_total / (count * WIDTH)
    return (query_grad, key_grad, value_grad, weight_grad, loss)


def solution(mesh):
    placed = (
        P("dp", "patch", None),
        P("dp", "patch", None),
        P("dp", "patch", None),
        P(),
        P("dp", "patch", None),
        P("dp"),
        P("dp", "patch"),
    )
    return jax.shard_map(
        local,
        mesh=mesh,
        in_specs=placed,
        out_specs=(
            P("dp", "patch", None),
            P("dp", "patch", None),
            P("dp", "patch", None),
            P("patch", "dp"),
            P(),
        ),
        check_vma=False,
    )
```

profile of v0, /device:TPU:0, one launch (start us, length us, event | category | flops | bytes accessed | tf_op | source)
XLA Modules:
  0.0 159.6 jit_solution(11204417154055203809)
XLA Ops:
  7.2 0.0 copy-start
  7.2 0.0 reduce-scatter.5.cloned.1.call-start
  7.2 10.8 %all_gather.22 = bf16[1,512,576]{1,2,0:T(8,128)(2,1)} all-gather(bf16[1,128,576]{1,2,0:T(8,128)(2,1)} %param.8), channel_id=1, replica_groups=mesh['dp'=8,'patch'=4] {'patch'}, dimensions={1}, use_global_device_ids=true | all-gather | bytes 737280 | tf_op jit(solution)/shard_map/all_gather | solution.py:132
  18.0 5.2 %all_gather.21 = s32[1,512]{1,0:T(1,128)S(1)} all-gather(s32[1,128]{1,0:T(1,128)} %param.13), channel_id=1, replica_groups=mesh['dp'=8,'patch'=4] {'patch'}, dimensions={1}, use_global_device_ids=true | all-gather | bytes 2560 | tf_op jit(solution)/shard_map/all_gather | solution.py:118
  23.9 0.1 dynamic_slice.15
  24.0 0.1 broadcast_compare_fusion.1
  24.1 0.0 copy-start.4
  24.1 1.8 %fusion.26 = (f32[8,128]{1,0:T(8,128)S(1)}, f32[8,128,512]{2,1,0:T(8,128)S(1)}) fusion(bf16[128,8,72]{0,2,1:T(8,128)(2,1)} %bitcast.73, bf16[512,8,72]{0,2,1:T(8,128)(2,1)} %bitcast.66, pred[128,512]{1,0:T(8,128)(4,1)S(1)} %broadcast_compare_fusion.1), kind=kOutput, calls=%fused_computation.48 | convolution fusion | flops 77069312 | bytes 2904064 | tf_op jit(solution)/shard_map/while/body/eval_jaxpr/qhe,khe->hqk/dot_general | solution.py:57
  25.9 0.7 fusion.2
  26.6 0.0 copy-done.4
  26.6 7.7 %all_gather.23 = bf16[1,512,576]{1,2,0:T(8,128)(2,1)S(1)} all-gather(bf16[1,128,576]{1,2,0:T(8,128)(2,1)S(1)} %copy-done.4), channel_id=1, replica_groups=mesh['dp'=8,'patch'=4] {'patch'}, dimensions={1}, use_global_device_ids=true | all-gather | bytes 737280 | tf_op jit(solution)/shard_map/all_gather | solution.py:133
  34.3 0.0 copy-start.6
  34.3 0.0 copy-start.7
  34.3 0.6 fusion.9
  34.9 0.2 copy-done.6
  35.1 0.0 copy-start.3
  35.1 0.0 copy-done
  35.1 0.3 copy-done.7
  35.4 1.1 multiply_reduce_fusion
  36.6 0.0 copy-start.1
  36.6 0.0 copy-done.3
  36.6 0.8 copy-done.1
  37.4 1.6 convolution_convert_fusion
  38.9 0.0 reduce-scatter.5.cloned.1.call-update
  39.0 0.0 reduce-scatter.7.cloned.1.call-start
  39.0 22.2 %psum.14 = f32[]{:T(128)} all-reduce(f32[]{:T(128)S(6)} %convert_element_type.57), channel_id=1, replica_groups=mesh['dp'=8,'patch'=4] {'dp'}, use_global_device_ids=true, to_apply=%region_3.4 | all-reduce | flops 1 | bytes 8 | tf_op jit(solution)/shard_map/psum | solution.py:115
  61.9 0.0 copy-start.8
  61.9 5.3 %all_gather.25 = f32[8,512]{1,0:T(8,128)S(1)} all-gather(f32[8,128]{1,0:T(8,128)S(1)} %get-tuple-element.46), channel_id=1, replica_groups=mesh['dp'=8,'patch'=4] {'patch'}, dimensions={1}, use_global_device_ids=true | all-gather | bytes 20480 | tf_op jit(solution)/shard_map/all_gather | solution.py:171
  67.2 7.8 %all_gather.24 = bf16[1,512,576]{1,2,0:T(8,128)(2,1)S(1)} all-gather(bf16[1,128,576]{1,2,0:T(8,128)(2,1)} %param.7), channel_id=1, replica_groups=mesh['dp'=8,'patch'=4] {'patch'}, dimensions={1}, use_global_device_ids=true | all-gather | bytes 737280 | tf_op jit(solution)/shard_map/all_gather | solution.py:184
  75.1 0.0 copy-start.2
  75.1 2.5 %convert_multiply_fusion = (f32[128,576]{0,1:T(8,128)}, bf16[128,576]{0,1:T(8,128)(2,1)S(1)}) fusion(bf16[128,8,72]{0,2,1:T(8,128)(2,1)} %copy-done.3, bf16[576,1152]{1,0:T(8,128)(2,1)S(1)} %copy-done, f32[128,1152]{1,0:T(8,128)} %copy-done.1), kind=kOutput, calls=%fused_computation.31 | convolution fusion | flops 170459136 | bytes 2506752 | tf_op jit(solution)/shard_map/td,fd->tf/dot_general | solution.py:144
  77.6 0.7 copy-done.5
  78.3 8.1 %all-gather = bf16[512,576]{0,1:T(8,128)(2,1)} all-gather(bf16[128,576]{0,1:T(8,128)(2,1)S(1)} %get-tuple-element.62), channel_id=2, replica_groups=mesh['dp'=8,'patch'=4] {'patch'}, dimensions={0}, use_global_device_ids=true | all-gather | bytes 737280 | tf_op jit(solution)/shard_map/all_gather | solution.py:185
  86.3 0.1 broadcast_compare_fusion
  86.5 0.0 copy-done.2
  86.5 0.0 copy-done.8
  86.5 2.1 %exponential_select_fusion = f32[8,512,128]{2,1,0:T(8,128)} fusion(bf16[512,8,72]{0,2,1:T(8,128)(2,1)S(1)} %bitcast.68, bf16[128,8,72]{0,2,1:T(8,128)(2,1)S(1)} %bitcast.80, f32[8,512]{1,0:T(8,128)S(1)} %all_gather.25, pred[512,128]{1,0:T(8,128)(4,1)S(1)} %broadcast_compare_fusion), kind=kOutput, calls=%fused_computation.4 | convolution fusion | flops 77594624 | bytes 2916352 | tf_op jit(solution)/shard_map/qhe,khe->hqk/dot_general | solution.py:77
  88.7 2.0 %copy.12 = bf16[144,1152]{0,1:T(8,128)(2,1)} copy(bf16[144,1152]{1,0:T(8,128)(2,1)} %reduce-scatter.5.cloned.1.call-done) | data formatting | bytes 663552
  90.7 0.0 reduce-scatter.7.cloned.1.call-update
  90.7 2.8 %convolution_multiply_fusion = f32[8,72,128]{2,1,0:T(8,128)} fusion(bf16[512,8,72]{0,2,1:T(8,128)(2,1)} %bitcast.63, f32[8,512,128]{2,1,0:T(8,128)} %exponential_select_fusion, f32[]{:T(128)S(6)} %div.19), kind=kOutput, calls=%fused_computation.13 | convolution fusion | flops 76095488 | bytes 2981892 | tf_op jit(solution)/shard_map/hqk,qhe->khe/dot_general | solution.py:82
  93.6 37.2 %psum.15 = f32[]{:T(128)} all-reduce(f32[]{:T(128)} %get-tuple-element.63), channel_id=1, replica_groups=mesh['dp'=8,'patch'=4] {'dp','patch'}, use_global_device_ids=true, to_apply=%region_7.8 | all-reduce | flops 1 | bytes 8 | tf_op jit(solution)/shard_map/psum | solution.py:188
  131.4 1.0 reduce_sum.32
  133.1 5.7 %all_gather.27 = f32[8,512]{1,0:T(8,128)S(1)} all-gather(f32[8,128]{1,0:T(8,128)S(1)} %bitcast.83), channel_id=1, replica_groups=mesh['dp'=8,'patch'=4] {'patch'}, dimensions={1}, use_global_device_ids=true | all-gather | bytes 20480 | tf_op jit(solution)/shard_map/all_gather | solution.py:172
  138.8 3.7 %fusion.5 = f32[8,128,72]{1,2,0:T(8,128)} fusion(bf16[512,8,72]{0,2,1:T(8,128)(2,1)} %bitcast.69, f32[8,512,128]{2,1,0:T(8,128)} %exponential_select_fusion, bf16[512,8,72]{0,2,1:T(8,128)(2,1)} %bitcast.64, bf16[128,8,72]{0,2,1:T(8,128)(2,1)} %bitcast.74, f32[8,512]{1,0:T(8,128)S(1)} %all_gather.27, f32[]{:T(128)S(6)} %mul.109), kind=kOutput, calls=%fused_computation.12 | convolution fusion | flops 152641536 | bytes 3735556 | tf_op jit(solution)/shard_map/hqk,qhe->khe/dot_general | solution.py:88
  142.5 3.1 %fusion.8 = f32[8,128,72]{1,2,0:T(8,128)} fusion(bf16[512,8,72]{0,2,1:T(8,128)(2,1)} %bitcast.67, f32[8,128,512]{2,1,0:T(8,128)S(1)} %get-tuple-element.49, bf16[128,8,72]{0,2,1:T(8,128)(2,1)} %bitcast.75, bf16[512,8,72]{0,2,1:T(8,128)(2,1)} %bitcast.77, f32[8,128]{1,0:T(8,128)S(1)} %bitcast.84, f32[8,128]{1,0:T(8,128)S(1)} %get-tuple-element.46, ...), kind=kOutput, calls=%fused_computation.17 | convolution fusion | flops 153690112 | bytes 3792900 | tf_op jit(solution)/shard_map/while/body/eval_jaxpr/hqk,khe->qhe/dot_general | solution.py:66
  145.7 4.3 %reduce-scatter.7.cloned.1.call-done = bf16[144,144]{1,0:T(8,128)(2,1)} async-done(((bf16[1152,144]{1,0:T(8,128)(2,1)}), bf16[144,144]{1,0:T(8,128)(2,1)}) %reduce-scatter.7.cloned.1.call-update) | async-done | bytes 41488
  149.9 1.0 copy.13
  150.9 0.7 convert_multiply_fusion.1
  (8 shorter events, 0.0 us)
Async XLA Ops:
  7.2 27.9 %copy-start = (bf16[576,1152]{1,0:T(8,128)(2,1)S(1)}, bf16[576,1152]{1,0:T(8,128)(2,1)}, u32[]{:S(2)}) copy-start(bf16[576,1152]{1,0:T(8,128)(2,1)} %param.10) | copy-start | bytes 3981316
  7.2 81.5 %reduce-scatter.5.cloned.1.call-start = ((), (), s32[]{:S(2)}) async-start(), calls=%async_computation.2 | async-start | bytes 1658880 | tf_op jit(solution)/shard_map/reduce_scatter | solution.py:189
  24.1 2.5 %copy-start.4 = (bf16[1,128,576]{1,2,0:T(8,128)(2,1)S(1)}, bf16[1,128,576]{1,2,0:T(8,128)(2,1)}, u32[]{:S(2)}) copy-start(bf16[1,128,576]{1,2,0:T(8,128)(2,1)} %param.9) | copy-start | bytes 442372
  34.3 0.8 copy-start.6
  34.3 1.2 copy-start.7
  35.1 1.5 copy-start.3
  36.6 0.8 copy-start.1
  39.0 111.0 %reduce-scatter.7.cloned.1.call-start = ((), (), s32[]{:S(2)}) async-start(), calls=%async_computation.3 | async-start | bytes 663552
  61.9 24.6 %copy-start.8 = (bf16[1,128,576]{1,2,0:T(8,128)(2,1)S(1)}, bf16[1,128,576]{1,2,0:T(8,128)(2,1)}, u32[]{:S(2)}) copy-start(bf16[1,128,576]{1,2,0:T(8,128)(2,1)} %param.8) | copy-start | bytes 442372
  75.1 11.4 %copy-start.2 = (bf16[1,512,576]{1,2,0:T(8,128)(2,1)}, bf16[1,512,576]{1,2,0:T(8,128)(2,1)S(1)}, u32[]{:S(2)}) copy-start(bf16[1,512,576]{1,2,0:T(8,128)(2,1)S(1)} %all_gather.24) | copy-start | bytes 1769476
  77.6 0.7 copy-start.5
Sparse Core Ops, SparseCore 0:
  39.1 26.9 reduce-scatter.4
  90.8 59.0 reduce-scatter.6
where the time goes:
time: 160 us
  blocking collectives  110 us (69%)
  matrix products  19.5 us (12%)
  between operations  18 us (11%)
  local copies, waits for them, and re-layouts  5.1 us (3%)
  waiting for transfers between devices  4.32 us (3%)
  other arithmetic  2.62 us (2%)
    psum x1, blocking collectives, local(): loss_total = lax.psum(loss_part, ('dp', 'patch'))  37.2 us
    psum x1, blocking collectives, local(): count = lax.psum(length.astype(jnp.float32), 'dp')  22.2 us
    all_gather x1, blocking collectives, local(): lax.all_gather(key_rows, 'patch', axis=1, tiled=True)  10.8 us
    all_gather x1, blocking collectives, local(): lax.all_gather(grad_attn[None], 'patch', axis=1, tiled=True)  8.09 us
    all_gather x1, blocking collectives, local(): lax.all_gather(query_rows, 'patch', axis=1, tiled=True)  7.85 us
    all_gather x1, blocking collectives, local(): lax.all_gather(value_rows, 'patch', axis=1, tiled=True)  7.65 us
    all_gather x1, blocking collectives, local(): lax.all_gather(delta, 'patch', axis=1, tiled=True)  5.74 us
    all_gather x1, blocking collectives, local(): lax.all_gather(log_norm, 'patch', axis=1, tiled=True)  5.34 us
  transfers between devices with their start and end apart: 2, of which 1 were waited for; matrix products, arithmetic and copies ran while one was open for 10% of the time, Pallas kernels for 0%

commit v1 on v0

v1 whole, which is shorter than its diff:
```python
import functools
import math

import jax
import jax.numpy as jnp
from jax import lax
from jax.experimental import pallas as pl
from jax.experimental.pallas import tpu as pltpu
from jax.sharding import PartitionSpec as P

MESH = pl.DeviceIdType.MESH
WIDTH = 1152
HEADS = 8
HEAD_DIM = 72
FEAT = 576
PAIRS = HEADS // 2
NEG_LARGE = -1e30
F32 = jnp.float32
BF16 = jnp.bfloat16
KEY, VALUE, QUERY, GRAD = range(4)


def window(pair):
    low = (2 * HEAD_DIM * pair) // 128 * 128
    return low, min(low + 256, FEAT)


def lane_mask(head, low, high):
    lane = low + lax.broadcasted_iota(jnp.int32, (1, high - low), 1)
    first = head * HEAD_DIM
    return ((lane >= first) & (lane < first + HEAD_DIM)).astype(F32)


def nt(left, right):
    return lax.dot_general(left, right, (((1,), (1,)), ((), ())), preferred_element_type=F32)


def nn(left, right):
    return lax.dot_general(left, right, (((1,), (0,)), ((), ())), preferred_element_type=F32)


def tn(left, right):
    return lax.dot_general(left, right, (((0,), (0,)), ((), ())), preferred_element_type=F32)


def kernel(
    members,
    groups,
    len_ref,
    seg_ref,
    q_ref,
    k_ref,
    v_ref,
    w_hbm,
    t_hbm,
    dq_ref,
    dk_ref,
    dv_ref,
    dw_ref,
    loss_ref,
    w_ref,
    t_ref,
    all_ref,
    seg_own,
    seg_all,
    stat_own,
    stat_all,
    stat_rows,
    bias_ref,
    prob_ref,
    attn_ref,
    dout_ref,
    part_ref,
    w1_ref,
    keep_ref,
    wx_ref,
    w2_ref,
    wz_ref,
    w3_ref,
    fin_ref,
    w4_ref,
    tile_own,
    tile_all,
    sum_own,
    sum_all,
    load_sem,
    send_sem,
    recv_sem,
    seg_send,
    seg_recv,
    stat_send,
    stat_recv,
    tile_send,
    tile_recv,
    sum_send,
    sum_recv,
    s1,
    r1,
    s2,
    r2,
    s3,
    r3,
    s4,
    r4,
):
    rows = q_ref.shape[0]
    total = rows * members
    chips = members // 2
    half = groups // 2
    outer = groups // 2
    mine = outer // 2
    me = lax.axis_index("patch")
    dp = lax.axis_index("dp")
    chip, core = me // 2, me % 2
    step_a, step_b = dp // 2, dp % 2
    partner = chip * 2 + 1 - core

    def patch_peer(shift):
        return lax.rem(me + shift, members)

    def dp_peer(shift):
        return lax.rem(dp + shift, groups)

    def far(shift):
        return lax.rem(chip + shift, chips)

    loads = [
        pltpu.make_async_copy(w_hbm, w_ref, load_sem.at[0]),
        pltpu.make_async_copy(t_hbm, t_ref, load_sem.at[1]),
    ]
    for load in loads:
        load.start()

    barrier = pltpu.get_barrier_semaphore()
    for shift in range(1, members):
        pl.semaphore_signal(barrier, inc=1, device_id=(dp, patch_peer(shift)), device_id_type=MESH)
    for shift in range(1, groups):
        pl.semaphore_signal(barrier, inc=1, device_id=(dp_peer(shift), me), device_id_type=MESH)
    seg_own[...] = jnp.broadcast_to(seg_ref[...], seg_own.shape)
    pl.semaphore_wait(barrier, members + groups - 2)

    def copy(src, dst, send, recv, device):
        return pltpu.make_async_remote_copy(
            src_ref=src, dst_ref=dst, send_sem=send, recv_sem=recv, device_id=device, device_id_type=MESH
        )

    pending = []

    def start(item):
        item.start()
        pending.append(item)

    def spread(array, src):
        dst = all_ref.at[array, me]
        for shift in range(1, chips):
            start(copy(src, dst, send_sem.at[array, shift], recv_sem.at[array, me], (dp, far(shift) * 2 + core)))
        start(copy(src, dst, send_sem.at[array, 0], recv_sem.at[array, me], (dp, partner)))

    def arrived(array, owner):
        slot = all_ref.at[array, owner]
        return copy(slot, slot, send_sem.at[array, 0], recv_sem.at[array, owner], (dp, partner)).wait_recv()

    def relay(array):
        for shift in range(1, chips):
            owner = far(shift) * 2 + core
            arrived(array, owner)
            slot = all_ref.at[array, owner]
            start(copy(slot, slot, send_sem.at[array, chips - 1 + shift], recv_sem.at[array, owner], (dp, partner)))

    def finish(array):
        arrived(array, partner)
        for shift in range(1, chips):
            arrived(array, far(shift) * 2 + 1 - core)

    def small(own, everyone, send, recv):
        for shift in range(1, members):
            start(copy(own, everyone.at[me], send.at[shift], recv.at[me], (dp, patch_peer(shift))))

    def small_wait(own, everyone, send, recv):
        for shift in range(1, members):
            owner = patch_peer(shift)
            copy(own, everyone.at[owner], send.at[shift], recv.at[owner], (dp, owner)).wait_recv()

    small(seg_own, seg_all, seg_send, seg_recv)
    spread(KEY, k_ref)
    spread(VALUE, v_ref)
    spread(QUERY, q_ref)
    all_ref[KEY, me] = k_ref[...]
    all_ref[VALUE, me] = v_ref[...]
    all_ref[QUERY, me] = q_ref[...]
    seg_all[me] = seg_own[...]

    masks = [
        [lane_mask(2 * pair + side, *window(pair)) for side in (0, 1)] for pair in range(PAIRS)
    ]

    def stacked(value, pair):
        low, high = window(pair)
        part = value[:, low:high]
        return jnp.concatenate(
            [part * masks[pair][0].astype(BF16), part * masks[pair][1].astype(BF16)], axis=0
        )

    def merged(value, pair):
        return value[:rows] * masks[pair][0] + value[rows:] * masks[pair][1]

    def whole(array, pair):
        low, high = window(pair)
        return all_ref[array, :, :, low:high].reshape(total, high - low)

    def put(out_ref, value, pair):
        low, high = window(pair)
        if pair == 0:
            out_ref[:, low:high] = value
        else:
            previous = window(pair - 1)[1]
            out_ref[:, low:previous] += value[:, : previous - low]
            out_ref[:, previous:high] = value[:, previous - low :]

    length = len_ref[0]
    small_wait(seg_own, seg_all, seg_send, seg_recv)
    seg_row = jnp.concatenate([seg_all[j][0:1] for j in range(members)], axis=1)
    position = lax.broadcasted_iota(jnp.int32, (1, total), 1)
    group_row = jnp.where(position < length, seg_row, -1).astype(F32)
    own_position = me * rows + lax.broadcasted_iota(jnp.int32, (rows, 1), 0)
    own_live = own_position < length
    wide_own = jnp.broadcast_to(seg_own[0:1].astype(F32), (rows, rows)).T
    own_column = jnp.where(own_live, wide_own[:, 0:1], -1.0)
    bias_ref[...] = jnp.where(own_column == group_row, 0.0, NEG_LARGE)

    log_scale = math.log2(math.e) / math.sqrt(HEAD_DIM)
    score_scale = 1.0 / math.sqrt(HEAD_DIM)

    def biased(scores):
        bias = bias_ref[...]
        return jnp.concatenate([scores[:rows] * log_scale + bias, scores[rows:] * log_scale + bias], axis=0)

    relay(KEY)
    finish(KEY)
    stats = []
    for pair in range(PAIRS):
        scores = biased(nt(stacked(q_ref[...], pair), whole(KEY, pair)))
        row_max = jnp.max(scores, axis=1, keepdims=True)
        probs = jnp.exp2(scores - row_max)
        denom = jnp.sum(probs, axis=1, keepdims=True)
        prob_ref[pair] = probs
        stats.append((row_max + jnp.log2(denom), denom))
    relay(VALUE)
    finish(VALUE)
    for pair in range(PAIRS):
        accum = nn(prob_ref[pair].astype(BF16), whole(VALUE, pair))
        put(attn_ref, merged(accum / stats[pair][1], pair), pair)
    attn_wide = attn_ref[...]
    attn = attn_wide.astype(BF16)
    loads[0].wait()
    loads[1].wait()
    output = nn(attn, w_ref[...])
    error = jnp.where(own_live, output - t_ref[...].astype(F32), 0.0)
    loss_part = jnp.sum(jnp.sum(error * error, axis=0, keepdims=True), axis=1, keepdims=True)
    tile_own[...] = jnp.broadcast_to(loss_part, tile_own.shape)
    dout_ref[...] = (2.0 * error).astype(BF16)
    grad_attn = nt(dout_ref[...], w_ref[...]).astype(BF16)
    all_ref[GRAD, me] = grad_attn
    relay(QUERY)
    spread(GRAD, all_ref.at[GRAD, me])
    small(tile_own, tile_all, tile_send, tile_recv)

    product = grad_attn.astype(F32) * attn.astype(F32)
    lane = lax.broadcasted_iota(jnp.int32, (rows, 128), 1)
    stat = jnp.zeros((rows, 128), F32)
    deltas = []
    for pair in range(PAIRS):
        low, high = window(pair)
        for side in (0, 1):
            head = 2 * pair + side
            delta = jnp.sum(product[:, low:high] * masks[pair][side], axis=1, keepdims=True)
            deltas.append(delta)
            log_norm = stats[pair][0][side * rows : (side + 1) * rows]
            stat = jnp.where(lane == head, log_norm, stat)
            stat = jnp.where(lane == HEADS + head, delta, stat)
    stat_own[...] = stat.T[: 2 * HEADS]
    small(stat_own, stat_all, stat_send, stat_recv)
    stat_all[me] = stat_own[...]

    share = WIDTH // groups
    part = tn(dout_ref[...], attn)
    for block in range(groups):
        part_ref[block] = part[block * share : (block + 1) * share].astype(BF16)
    first = core * half
    other = (1 - core) * half
    stage1 = copy(part_ref.at[pl.ds(other, half)], w1_ref, s1, r1, (dp, partner))
    start(stage1)

    def query_pass(pair):
        delta = jnp.concatenate([deltas[2 * pair], deltas[2 * pair + 1]], axis=0)
        dprobs = nt(stacked(grad_attn, pair), whole(VALUE, pair))
        dscores = prob_ref[pair] * (1.0 / stats[pair][1]) * (dprobs - delta)
        value = nn(dscores.astype(BF16), whole(KEY, pair))
        put(dq_ref, merged(value, pair) * score_scale, pair)

    query_pass(0)
    query_pass(1)

    stage1.wait_recv()
    stage2 = []
    for i in range(mine):
        away = 2 * i + 1 - step_b
        near = 2 * i + step_b
        wx_ref[i] = (part_ref[first + away].astype(F32) + w1_ref[away].astype(F32)).astype(BF16)
        item = copy(wx_ref.at[i], w2_ref.at[i], s2.at[i], r2.at[i], (step_a * 2 + 1 - step_b, me))
        start(item)
        stage2.append(item)
        keep_ref[i] = part_ref[first + near].astype(F32) + w1_ref[near].astype(F32)

    relay(GRAD)
    query_pass(2)
    query_pass(3)
    finish(QUERY)
    finish(GRAD)
    small_wait(stat_own, stat_all, stat_send, stat_recv)
    stat_rows[...] = jnp.concatenate([stat_all[j] for j in range(members)], axis=1)

    def key_pass(pair):
        def spread_rows(base):
            return jnp.concatenate(
                [
                    jnp.broadcast_to(stat_rows[base + 2 * pair + side : base + 2 * pair + side + 1, :], (rows, total))
                    for side in (0, 1)
                ],
                axis=0,
            )

        queries = whole(QUERY, pair)
        grads = whole(GRAD, pair)
        scores = biased(nt(stacked(k_ref[...], pair), queries))
        probs = jnp.exp2(scores - spread_rows(0))
        put(dv_ref, merged(nn(probs.astype(BF16), grads), pair), pair)
        dprobs = nt(stacked(v_ref[...], pair), grads)
        dscores = (probs * (dprobs - spread_rows(HEADS))).astype(BF16)
        put(dk_ref, merged(nn(dscores, queries), pair) * score_scale, pair)

    def third(i):
        stage2[i].wait_recv()
        wz_ref[i] = (keep_ref[i] + w2_ref[i].astype(F32)).astype(BF16)
        owner = core * mine + i
        item = copy(wz_ref.at[i], w3_ref.at[step_a], s3.at[i], r3.at[step_a], (owner * 2 + step_b, me))

        @pl.when(owner != step_a)
        def _():
            item.start()

        return owner, item

    key_pass(0)
    stage3 = [third(0)]
    key_pass(1)
    stage3 += [third(i) for i in range(1, mine)]

    small_wait(tile_own, tile_all, tile_send, tile_recv)
    tile_all[me] = tile_own[...]
    pack_loss = tile_all[0]
    for j in range(1, members):
        pack_loss = pack_loss + tile_all[j]
    tile_lane = lax.broadcasted_iota(jnp.int32, pack_loss.shape, 1)
    sum_own[...] = jnp.where(tile_lane == 0, pack_loss, length.astype(F32))
    for shift in range(1, groups):
        start(copy(sum_own, sum_all.at[dp], sum_send.at[shift], sum_recv.at[dp], (dp_peer(shift), me)))
    sum_all[dp] = sum_own[...]

    key_pass(2)

    collect = step_a // mine
    is_collector = core == collect
    stage4 = [
        copy(fin_ref, w4_ref.at[chip], s4.at[shift], r4.at[chip], (dp, patch_peer(shift)))
        for shift in range(1, members)
    ]

    @pl.when(is_collector)
    def _():
        summed = wz_ref[step_a - core * mine].astype(F32)
        for shift in range(1, outer):
            source = lax.rem(step_a + shift, outer)
            copy(wz_ref.at[0], w3_ref.at[source], s3.at[0], r3.at[source], (source * 2 + step_b, me)).wait_recv()
            summed = summed + w3_ref[source].astype(F32)
        fin_ref[...] = summed.astype(BF16)
        for item in stage4:
            item.start()
        w4_ref[chip] = fin_ref[...]

    key_pass(3)

    for shift in range(1, groups):
        source = dp_peer(shift)
        copy(sum_own, sum_all.at[source], sum_send.at[shift], sum_recv.at[source], (source, me)).wait_recv()
    totals = sum_all[0]
    for j in range(1, groups):
        totals = totals + sum_all[j]
    count = totals[0:1, 1:2]
    ratio = (groups * total) / count
    loss_ref[...] = jnp.broadcast_to(totals[0:1, 0:1] / (count * WIDTH), loss_ref.shape)
    dq_ref[...] = dq_ref[...] * ratio
    dk_ref[...] = dk_ref[...] * ratio
    dv_ref[...] = dv_ref[...] * ratio

    def fetched(owner):
        copy(fin_ref, w4_ref.at[owner], s4.at[0], r4.at[owner], (dp, partner)).wait_recv()

    @pl.when(jnp.logical_not(is_collector))
    def _():
        fetched(chip)

    for shift in range(1, chips):
        fetched(far(shift))
    features = dw_ref.shape[0]
    chosen = (
        lax.broadcasted_iota(jnp.int32, (features, FEAT), 1)
        == me * features + lax.broadcasted_iota(jnp.int32, (features, FEAT), 0)
    ).astype(F32).astype(BF16)
    result = nt(chosen, w4_ref[0])
    for j in range(1, chips):
        result = result + nt(chosen, w4_ref[j])
    dw_ref[...] = result * (ratio / total)

    for item in pending:
        item.wait_send()
    for owner, item in stage3:

        @pl.when(owner != step_a)
        def _():
            item.wait_send()

    @pl.when(is_collector)
    def _():
        for item in stage4:
            item.wait_send()


def solution(mesh):
    members, groups = mesh.shape["patch"], mesh.shape["dp"]

    def local(query_rows, key_rows, value_rows, out_weight, target, lengths, segments):
        rows = query_rows.shape[1]
        total = rows * members
        chips = members // 2
        outer = groups // 2
        mine = outer // 2
        share = WIDTH // groups
        vmem = pl.BlockSpec(memory_space=pltpu.VMEM)
        hbm = pl.BlockSpec(memory_space=pl.ANY)
        dma = pltpu.SemaphoreType.DMA
        outs = pl.pallas_call(
            functools.partial(kernel, members, groups),
            out_shape=(
                jax.ShapeDtypeStruct((rows, FEAT), F32),
                jax.ShapeDtypeStruct((rows, FEAT), F32),
                jax.ShapeDtypeStruct((rows, FEAT), F32),
                jax.ShapeDtypeStruct((FEAT // members, share), F32),
                jax.ShapeDtypeStruct((8, 128), F32),
            ),
            in_specs=[pl.BlockSpec(memory_space=pltpu.SMEM), vmem, vmem, vmem, vmem, hbm, hbm],
            out_specs=(vmem,) * 5,
            scratch_shapes=[
                pltpu.VMEM((FEAT, WIDTH), BF16),
                pltpu.VMEM((rows, WIDTH), BF16),
                pltpu.VMEM((4, members, rows, FEAT), BF16),
                pltpu.VMEM((8, rows), jnp.int32),
                pltpu.VMEM((members, 8, rows), jnp.int32),
                pltpu.VMEM((2 * HEADS, rows), F32),
                pltpu.VMEM((members, 2 * HEADS, rows), F32),
                pltpu.VMEM((2 * HEADS, total), F32),
                pltpu.VMEM((rows, total), F32),
                pltpu.VMEM((PAIRS, 2 * rows, total), F32),
                pltpu.VMEM((rows, FEAT), F32),
                pltpu.VMEM((rows, WIDTH), BF16),
                pltpu.VMEM((groups, share, FEAT), BF16),
                pltpu.VMEM((groups // 2, share, FEAT), BF16),
                pltpu.VMEM((mine, share, FEAT), F32),
                pltpu.VMEM((mine, share, FEAT), BF16),
                pltpu.VMEM((mine, share, FEAT), BF16),
                pltpu.VMEM((mine, share, FEAT), BF16),
                pltpu.VMEM((outer, share, FEAT), BF16),
                pltpu.VMEM((share, FEAT), BF16),
                pltpu.VMEM((chips, share, FEAT), BF16),
                pltpu.VMEM((8, 128), F32),
                pltpu.VMEM((members, 8, 128), F32),
                pltpu.VMEM((8, 128), F32),
                pltpu.VMEM((groups, 8, 128), F32),
                dma((2,)),
                dma((4, members)),
                dma((4, members)),
                dma((members,)),
                dma((members,)),
                dma((members,)),
                dma((members,)),
                dma((members,)),
                dma((members,)),
                dma((groups,)),
                dma((groups,)),
                dma,
                dma,
                dma((mine,)),
                dma((mine,)),
                dma((mine,)),
                dma((outer,)),
                dma((members,)),
                dma((chips,)),
            ],
            compiler_params=pltpu.CompilerParams(collective_id=0, has_side_effects=True),
            name="sublayer",
        )(lengths, segments, query_rows[0], key_rows[0], value_rows[0], out_weight, target[0])
        return (outs[0][None], outs[1][None], outs[2][None], outs[3], outs[4][0, 0])

    placed = (
        P("dp", "patch", None),
        P("dp", "patch", None),
        P("dp", "patch", None),
        P(),
        P("dp", "patch", None),
        P("dp"),
        P("dp", "patch"),
    )
    return jax.shard_map(
        local,
        mesh=mesh,
        in_specs=placed,
        out_specs=(
            P("dp", "patch", None),
            P("dp", "patch", None),
            P("dp", "patch", None),
            P("patch", "dp"),
            P(),
        ),
        check_vma=False,
    )
```

time: 160 us -> 58.6 us (0.37)
  the two profiles are of different devices: /device:TPU:0 before, /device:TPU:9 now
where the time goes in v1:
time: 58.6 us; the launch traced here: 58.3 us
  Pallas kernels  45.4 us (77%)
  local copies, waits for them, and re-layouts  11.6 us (20%)
  between operations  1.31 us (2%)
    pallas_call x1, Pallas kernels, local(): pl.pallas_call(functools.partial(kernel, members, groups), out_shape=(jax...  45.4 us
    unnamed x11, local copies, waits for them, and re-layouts  10.3 us
    slice x1, local copies, waits for them, and re-layouts, local(): return (outs[0][None], outs[1][None], outs[2][None], outs[3], outs[4][0, 0])  1.24 us

profile of v1, /device:TPU:9, one launch (start us, length us, event | category | flops | bytes accessed | tf_op | source)
XLA Modules:
  0.0 58.3 jit_solution(4238544769053109802)
XLA Ops:
  1.3 1.7 %copy.12 = bf16[1,128,576]{2,1,0:T(8,128)(2,1)} copy(bf16[1,128,576]{1,2,0:T(8,128)(2,1)} %param.7) | data formatting | bytes 294912 | tf_op args[0]
  3.0 1.7 %copy.13 = bf16[1,128,576]{2,1,0:T(8,128)(2,1)} copy(bf16[1,128,576]{1,2,0:T(8,128)(2,1)} %param.8) | data formatting | bytes 294912 | tf_op args[1]
  4.7 1.7 %copy.14 = bf16[1,128,576]{2,1,0:T(8,128)(2,1)} copy(bf16[1,128,576]{1,2,0:T(8,128)(2,1)} %param.9) | data formatting | bytes 294912 | tf_op args[2]
  6.4 45.4 %sublayer.1 = (f32[128,576]{1,0:T(8,128)}, f32[128,576]{1,0:T(8,128)}, f32[128,576]{1,0:T(8,128)}, f32[144,144]{1,0:T(8,128)}, f32[8,128]{1,0:T(8,128)}) custom-call(s32[1]{0:T(128)S(6)} %copy.19.len_ref, s32[1,128]{1,0:T(1,128)} %seg_ref.1, bf16[128,576]{1,0:T(8,128)(2,1)} %bitcast.8, bf16[128,576]{1,0:T(8,128)(2,1)} %bitcast.9, bf16[128,576]{1,0:T(8,128)(2,1)} %bitcast.10, ...), custom_call_target="tpu_custom_call" | custom-call | tf_op jit(solution)/shard_map/sublayer/pallas_call | solution.py:452
  51.9 0.0 copy-start
  51.9 0.0 copy-start.1
  51.9 1.2 %slice.3 = f32[1,1]{1,0:T(1,128)} slice(f32[8,128]{1,0:T(8,128)} %get-tuple-element.14), slice={[0:1], [0:1]} | slice | bytes 8 | tf_op jit(solution)/shard_map/slice | solution.py:512
  53.1 1.8 %copy.15 = f32[1,128,576]{1,2,0:T(8,128)} copy(f32[1,128,576]{2,1,0:T(8,128)} %bitcast.13) | data formatting | bytes 589824
  55.0 1.8 %copy.16 = f32[1,128,576]{1,2,0:T(8,128)} copy(f32[1,128,576]{2,1,0:T(8,128)} %bitcast.12) | data formatting | bytes 589824
  56.8 0.0 copy-done
  56.8 0.9 %copy.17 = f32[1,128,576]{1,2,0:T(8,128)} copy(f32[1,128,576]{2,1,0:T(8,128)S(1)} %bitcast.11) | data formatting | bytes 589824
  57.7 0.0 copy-done.1
  57.7 0.7 %copy.20 = f32[144,144]{1,0:T(8,128)} copy(f32[144,144]{1,0:T(8,128)S(1)} %copy-done.1) | data formatting | bytes 165888
Async XLA Ops:
  51.9 4.9 %copy-start = (f32[128,576]{1,0:T(8,128)S(1)}, f32[128,576]{1,0:T(8,128)}, u32[]{:S(2)}) copy-start(f32[128,576]{1,0:T(8,128)} %get-tuple-element.12) | copy-start | bytes 884740
  51.9 5.8 %copy-start.1 = (f32[144,144]{1,0:T(8,128)S(1)}, f32[144,144]{1,0:T(8,128)}, u32[]{:S(2)}) copy-start(f32[144,144]{1,0:T(8,128)} %get-tuple-element.28) | copy-start | bytes 248836

commit v2 on v1

v2 whole, which is shorter than its diff:
```python
import functools
import math

import jax
import jax.numpy as jnp
from jax import lax
from jax.experimental import pallas as pl
from jax.experimental.pallas import tpu as pltpu
from jax.sharding import PartitionSpec as P

MESH = pl.DeviceIdType.MESH
WIDTH = 1152
HEADS = 8
HEAD_DIM = 72
FEAT = 576
PAIRS = HEADS // 2
PAIR_ROWS = 2 * HEAD_DIM
FEAT_PAD = 640
SPAN = 256
NEG_LARGE = -1e30
F32 = jnp.float32
BF16 = jnp.bfloat16
KEY, VALUE, QUERY, GRAD = range(4)


def nt(left, right):
    return lax.dot_general(left, right, (((1,), (1,)), ((), ())), preferred_element_type=F32)


def nn(left, right):
    return lax.dot_general(left, right, (((1,), (0,)), ((), ())), preferred_element_type=F32)


def tn(left, right):
    return lax.dot_general(left, right, (((0,), (0,)), ((), ())), preferred_element_type=F32)


def span_start(owner, features):
    return pl.multiple_of(jnp.minimum(owner * features // 128 * 128, FEAT_PAD - SPAN), 128)


def kernel(
    members,
    groups,
    len_ref,
    seg_ref,
    q_ref,
    k_ref,
    v_ref,
    w_hbm,
    t_hbm,
    dq_ref,
    dk_ref,
    dv_ref,
    dw_ref,
    sum_ref,
    w_ref,
    t_ref,
    seg_row_ref,
    all_ref,
    seg_own,
    seg_all,
    stat_own,
    stat_all,
    stat_columns,
    bias_ref,
    prob_ref,
    attn_ref,
    dout_ref,
    part_ref,
    w1_ref,
    keep_ref,
    wx_ref,
    w2_ref,
    wz_ref,
    w3_ref,
    fin_ref,
    w4_ref,
    tile_own,
    tile_all,
    sum_own,
    sum_all,
    load_sem,
    send_sem,
    recv_sem,
    seg_send,
    seg_recv,
    stat_send,
    stat_recv,
    tile_send,
    tile_recv,
    sum_send,
    sum_recv,
    s1,
    r1,
    s2,
    r2,
    s3,
    r3,
    s4,
    r4,
):
    rows = q_ref.shape[1]
    total = rows * members
    chips = members // 2
    half = groups // 2
    outer = groups // 2
    mine = outer // 2
    features = dw_ref.shape[0]
    me = lax.axis_index("patch")
    dp = lax.axis_index("dp")
    chip, core = me // 2, me % 2
    step_a, step_b = dp // 2, dp % 2
    partner = chip * 2 + 1 - core

    def patch_peer(shift):
        return lax.rem(me + shift, members)

    def dp_peer(shift):
        return lax.rem(dp + shift, groups)

    def far(shift):
        return lax.rem(chip + shift, chips)

    loads = [
        pltpu.make_async_copy(seg_ref, seg_row_ref, load_sem.at[0]),
        pltpu.make_async_copy(k_ref, all_ref.at[KEY, me], load_sem.at[1]),
        pltpu.make_async_copy(v_ref, all_ref.at[VALUE, me], load_sem.at[2]),
        pltpu.make_async_copy(q_ref, all_ref.at[QUERY, me], load_sem.at[3]),
        pltpu.make_async_copy(w_hbm, w_ref, load_sem.at[4]),
        pltpu.make_async_copy(t_hbm, t_ref, load_sem.at[5]),
    ]
    for load in loads:
        load.start()

    barrier = pltpu.get_barrier_semaphore()
    for shift in range(1, members):
        pl.semaphore_signal(barrier, inc=1, device_id=(dp, patch_peer(shift)), device_id_type=MESH)
    for shift in range(1, groups):
        pl.semaphore_signal(barrier, inc=1, device_id=(dp_peer(shift), me), device_id_type=MESH)
    loads[0].wait()
    seg_own[...] = jnp.broadcast_to(seg_row_ref[...], seg_own.shape)
    seg_all[me] = seg_own[...]
    for load in loads[1:4]:
        load.wait()
    pl.semaphore_wait(barrier, members + groups - 2)

    def copy(src, dst, send, recv, device):
        return pltpu.make_async_remote_copy(
            src_ref=src, dst_ref=dst, send_sem=send, recv_sem=recv, device_id=device, device_id_type=MESH
        )

    pending = []

    def start(item):
        item.start()
        pending.append(item)

    def rows_of(pair):
        return pl.ds(PAIR_ROWS * pair, PAIR_ROWS)

    def spread(array, pair):
        src = dst = all_ref.at[array, me, rows_of(pair)]
        recv = recv_sem.at[array, me, pair]
        for shift in range(1, chips):
            start(copy(src, dst, send_sem.at[array, shift, pair], recv, (dp, far(shift) * 2 + core)))
        start(copy(src, dst, send_sem.at[array, 0, pair], recv, (dp, partner)))

    def arrived(array, owner, pair):
        slot = all_ref.at[array, owner, rows_of(pair)]
        copy(slot, slot, send_sem.at[array, 0, pair], recv_sem.at[array, owner, pair], (dp, partner)).wait_recv()

    def relay(array, pair):
        for shift in range(1, chips):
            owner = far(shift) * 2 + core
            arrived(array, owner, pair)
            slot = all_ref.at[array, owner, rows_of(pair)]
            send = send_sem.at[array, chips - 1 + shift, pair]
            start(copy(slot, slot, send, recv_sem.at[array, owner, pair], (dp, partner)))

    def finish(array, pair):
        arrived(array, partner, pair)
        for shift in range(1, chips):
            arrived(array, far(shift) * 2 + 1 - core, pair)

    def small(own, everyone, send, recv):
        for shift in range(1, members):
            start(copy(own, everyone.at[me], send.at[shift], recv.at[me], (dp, patch_peer(shift))))

    def small_wait(own, everyone, send, recv):
        for shift in range(1, members):
            owner = patch_peer(shift)
            copy(own, everyone.at[owner], send.at[shift], recv.at[owner], (dp, owner)).wait_recv()

    small(seg_own, seg_all, seg_send, seg_recv)
    for pair in range(PAIRS):
        spread(KEY, pair)
        spread(VALUE, pair)
    for pair in range(PAIRS):
        spread(QUERY, pair)

    upper = lax.broadcasted_iota(jnp.int32, (PAIR_ROWS, 1), 0) < HEAD_DIM
    masks = [upper.astype(F32).astype(BF16), jnp.logical_not(upper).astype(F32).astype(BF16)]

    def stacked(value):
        return jnp.concatenate([value * masks[0], value * masks[1]], axis=1)

    def merged(value):
        return jnp.concatenate([value[:HEAD_DIM, :rows], value[HEAD_DIM:, rows:]], axis=0)

    def part_of(ref, pair):
        return ref[PAIR_ROWS * pair : PAIR_ROWS * (pair + 1), :]

    def own(array, pair):
        return all_ref[array, me, PAIR_ROWS * pair : PAIR_ROWS * (pair + 1), :]

    def whole(array, pair):
        low = PAIR_ROWS * pair
        return jnp.concatenate([all_ref[array, j, low : low + PAIR_ROWS, :] for j in range(members)], axis=1)

    length = len_ref[0]
    lane_position = lax.broadcasted_iota(jnp.int32, (1, rows), 1)
    own_live = me * rows + lax.broadcasted_iota(jnp.int32, (rows, 1), 0) < length
    own_group = jnp.where(me * rows + lane_position < length, seg_own[0:1], -1).astype(F32)
    small_wait(seg_own, seg_all, seg_send, seg_recv)
    for j in range(members):
        group = jnp.where(j * rows + lane_position < length, seg_all[j][0:1], -1).astype(F32)
        group = jnp.broadcast_to(group, (rows, rows)).T
        bias_ref[j * rows : (j + 1) * rows, :] = jnp.where(group == own_group, 0.0, NEG_LARGE)
    attn_ref[FEAT:, :] = jnp.zeros((FEAT_PAD - FEAT, rows), F32)

    log_scale = math.log2(math.e) / math.sqrt(HEAD_DIM)
    score_scale = 1.0 / math.sqrt(HEAD_DIM)

    def biased(scores):
        bias = bias_ref[...]
        return scores * log_scale + jnp.concatenate([bias, bias], axis=1)

    denoms = []
    for pair in range(PAIRS):
        relay(KEY, pair)
        relay(VALUE, pair)
        finish(KEY, pair)
        scores = biased(tn(whole(KEY, pair), stacked(own(QUERY, pair))))
        row_max = jnp.max(scores, axis=0, keepdims=True)
        probs = jnp.exp2(scores - row_max)
        denom = jnp.sum(probs, axis=0, keepdims=True)
        prob_ref[pair] = probs
        log_norm = row_max + jnp.log2(denom)
        for side in (0, 1):
            head = 2 * pair + side
            stat_own[head : head + 1, :] = log_norm[:, side * rows : (side + 1) * rows]
        denoms.append(denom)
        finish(VALUE, pair)
        accum = nn(whole(VALUE, pair), probs.astype(BF16))
        attn_ref[PAIR_ROWS * pair : PAIR_ROWS * (pair + 1), :] = merged(accum / denom)

    attn = attn_ref[...].T.astype(BF16)
    loads[4].wait()
    loads[5].wait()
    output = nn(attn[:, :FEAT], w_ref[...])
    error = jnp.where(own_live, output - t_ref[...].astype(F32), 0.0)
    dout_ref[...] = (2.0 * error).astype(BF16)

    share = WIDTH // groups
    part = tn(dout_ref[...], attn)
    for block in range(groups):
        part_ref[block] = part[block * share : (block + 1) * share].astype(BF16)
    first = core * half
    other = (1 - core) * half
    stage1 = copy(part_ref.at[pl.ds(other, half)], w1_ref, s1, r1, (dp, partner))
    start(stage1)

    for pair in range(PAIRS):
        grad = nt(part_of(w_ref, pair), dout_ref[...]).astype(BF16)
        all_ref[GRAD, me, PAIR_ROWS * pair : PAIR_ROWS * (pair + 1), :] = grad
        spread(GRAD, pair)
        attn_pair = part_of(attn_ref, pair).astype(BF16).astype(F32)
        product = grad.astype(F32) * attn_pair
        for side in (0, 1):
            head = HEADS + 2 * pair + side
            stat_own[head : head + 1, :] = jnp.sum(
                product[HEAD_DIM * side : HEAD_DIM * (side + 1)], axis=0, keepdims=True
            )
    small(stat_own, stat_all, stat_send, stat_recv)
    stat_all[me] = stat_own[...]
    loss_part = jnp.sum(jnp.sum(error * error, axis=0, keepdims=True), axis=1, keepdims=True)
    tile_own[...] = jnp.broadcast_to(loss_part, tile_own.shape)
    small(tile_own, tile_all, tile_send, tile_recv)

    def query_pass(pair):
        low = HEADS + 2 * pair
        delta = jnp.concatenate([stat_own[low : low + 1, :], stat_own[low + 1 : low + 2, :]], axis=1)
        dprobs = tn(whole(VALUE, pair), stacked(own(GRAD, pair)))
        dscores = prob_ref[pair] * (1.0 / denoms[pair]) * (dprobs - delta)
        value = nn(whole(KEY, pair), dscores.astype(BF16))
        dq_ref[PAIR_ROWS * pair : PAIR_ROWS * (pair + 1), :] = merged(value) * score_scale

    stage1.wait_recv()
    stage2 = []
    for i in range(mine):
        away = 2 * i + 1 - step_b
        wx_ref[i] = (part_ref[first + away].astype(F32) + w1_ref[away].astype(F32)).astype(BF16)
        item = copy(wx_ref.at[i], w2_ref.at[i], s2.at[i], r2.at[i], (step_a * 2 + 1 - step_b, me))
        start(item)
        stage2.append(item)
    for i in range(mine):
        near = 2 * i + step_b
        keep_ref[i] = part_ref[first + near].astype(F32) + w1_ref[near].astype(F32)
    for pair in range(PAIRS):
        relay(QUERY, pair)

    query_pass(0)
    query_pass(1)
    relay(GRAD, 0)
    relay(GRAD, 1)
    small_wait(stat_own, stat_all, stat_send, stat_recv)
    for j in range(members):
        tall = jnp.concatenate([stat_all[j], jnp.zeros((128 - 2 * HEADS, rows), F32)], axis=0)
        stat_columns[j * rows : (j + 1) * rows, :] = tall.T

    def third(i):
        stage2[i].wait_recv()
        wz_ref[i] = (keep_ref[i] + w2_ref[i].astype(F32)).astype(BF16)
        owner = core * mine + i
        item = copy(wz_ref.at[i], w3_ref.at[step_a], s3.at[i], r3.at[step_a], (owner * 2 + step_b, me))

        @pl.when(owner != step_a)
        def _():
            item.start()

        return owner, item

    def key_pass(pair):
        def columns(base):
            low = base + 2 * pair
            return jnp.concatenate(
                [jnp.broadcast_to(stat_columns[:, low + side : low + side + 1], (total, rows)) for side in (0, 1)],
                axis=1,
            )

        finish(QUERY, pair)
        finish(GRAD, pair)
        queries = whole(QUERY, pair)
        grads = whole(GRAD, pair)
        scores = biased(tn(queries, stacked(own(KEY, pair))))
        probs = jnp.exp2(scores - columns(0))
        dv_ref[PAIR_ROWS * pair : PAIR_ROWS * (pair + 1), :] = merged(nn(grads, probs.astype(BF16)))
        dprobs = tn(grads, stacked(own(VALUE, pair)))
        dscores = (probs * (dprobs - columns(HEADS))).astype(BF16)
        dk_ref[PAIR_ROWS * pair : PAIR_ROWS * (pair + 1), :] = merged(nn(queries, dscores)) * score_scale

    stage3 = [third(0)]
    relay(GRAD, 2)
    relay(GRAD, 3)
    query_pass(2)
    stage3 += [third(i) for i in range(1, mine)]
    query_pass(3)

    small_wait(tile_own, tile_all, tile_send, tile_recv)
    tile_all[me] = tile_own[...]
    pack_loss = tile_all[0]
    for j in range(1, members):
        pack_loss = pack_loss + tile_all[j]
    tile_lane = lax.broadcasted_iota(jnp.int32, pack_loss.shape, 1)
    sum_own[...] = jnp.where(tile_lane == 0, pack_loss, length.astype(F32))
    for shift in range(1, groups):
        start(copy(sum_own, sum_all.at[dp], sum_send.at[shift], sum_recv.at[dp], (dp_peer(shift), me)))
    sum_all[dp] = sum_own[...]

    key_pass(0)
    key_pass(1)

    collect = step_a // mine
    is_collector = core == collect
    stage4 = []
    for shift in range(1, members):
        target = patch_peer(shift)
        span = fin_ref.at[:, pl.ds(span_start(target, features), SPAN)]
        stage4.append(copy(span, w4_ref.at[chip], s4.at[shift], r4.at[chip], (dp, target)))

    @pl.when(is_collector)
    def _():
        summed = wz_ref[step_a - core * mine].astype(F32)
        for shift in range(1, outer):
            source = lax.rem(step_a + shift, outer)
            copy(wz_ref.at[0], w3_ref.at[source], s3.at[0], r3.at[source], (source * 2 + step_b, me)).wait_recv()
            summed = summed + w3_ref[source].astype(F32)
        fin_ref[...] = summed.astype(BF16)
        for item in stage4:
            item.start()
        w4_ref[chip] = fin_ref[:, pl.ds(span_start(me, features), SPAN)]

    key_pass(2)
    key_pass(3)

    for shift in range(1, groups):
        source = dp_peer(shift)
        copy(sum_own, sum_all.at[source], sum_send.at[shift], sum_recv.at[source], (source, me)).wait_recv()
    totals = sum_all[0]
    for j in range(1, groups):
        totals = totals + sum_all[j]
    sum_ref[...] = totals

    def fetched(owner):
        copy(w4_ref.at[owner], w4_ref.at[owner], s4.at[0], r4.at[owner], (dp, partner)).wait_recv()

    @pl.when(jnp.logical_not(is_collector))
    def _():
        fetched(chip)

    for shift in range(1, chips):
        fetched(far(shift))
    shape = (features, SPAN)
    start_lane = me * features - span_start(me, features)
    chosen = (
        lax.broadcasted_iota(jnp.int32, shape, 1) == start_lane + lax.broadcasted_iota(jnp.int32, shape, 0)
    ).astype(F32).astype(BF16)
    result = nt(chosen, w4_ref[0])
    for j in range(1, chips):
        result = result + nt(chosen, w4_ref[j])
    dw_ref[...] = result

    for item in pending:
        item.wait_send()
    for owner, item in stage3:

        @pl.when(owner != step_a)
        def _():
            item.wait_send()

    @pl.when(is_collector)
    def _():
        for item in stage4:
            item.wait_send()


def scale_kernel(slots, total, sum_ref, dq_ref, dk_ref, dv_ref, dw_ref, query_ref, key_ref, value_ref, weight_ref, loss_ref):
    count = sum_ref[0:1, 1:2]
    ratio = slots / count
    query_ref[...] = dq_ref[...] * ratio
    key_ref[...] = dk_ref[...] * ratio
    value_ref[...] = dv_ref[...] * ratio
    weight_ref[...] = dw_ref[...] * (ratio / total)
    loss_ref[...] = sum_ref[0:1, 0:1] / (count * WIDTH)


def solution(mesh):
    members, groups = mesh.shape["patch"], mesh.shape["dp"]

    def local(query_rows, key_rows, value_rows, out_weight, target, lengths, segments):
        rows = query_rows.shape[1]
        total = rows * members
        chips = members // 2
        outer = groups // 2
        mine = outer // 2
        share = WIDTH // groups
        vmem = pl.BlockSpec(memory_space=pltpu.VMEM)
        hbm = pl.BlockSpec(memory_space=pltpu.HBM)
        dma = pltpu.SemaphoreType.DMA
        outs = pl.pallas_call(
            functools.partial(kernel, members, groups),
            out_shape=(
                jax.ShapeDtypeStruct((FEAT, rows), F32),
                jax.ShapeDtypeStruct((FEAT, rows), F32),
                jax.ShapeDtypeStruct((FEAT, rows), F32),
                jax.ShapeDtypeStruct((FEAT // members, share), F32),
                jax.ShapeDtypeStruct((8, 128), F32),
            ),
            in_specs=[pl.BlockSpec(memory_space=pltpu.SMEM)] + [hbm] * 6,
            out_specs=(vmem,) * 5,
            scratch_shapes=[
                pltpu.VMEM((FEAT, WIDTH), BF16),
                pltpu.VMEM((rows, WIDTH), BF16),
                pltpu.VMEM((1, rows), jnp.int32),
                pltpu.VMEM((4, members, FEAT, rows), BF16),
                pltpu.VMEM((8, rows), jnp.int32),
                pltpu.VMEM((members, 8, rows), jnp.int32),
                pltpu.VMEM((2 * HEADS, rows), F32),
                pltpu.VMEM((members, 2 * HEADS, rows), F32),
                pltpu.VMEM((total, 128), F32),
                pltpu.VMEM((total, rows), F32),
                pltpu.VMEM((PAIRS, total, 2 * rows), F32),
                pltpu.VMEM((FEAT_PAD, rows), F32),
                pltpu.VMEM((rows, WIDTH), BF16),
                pltpu.VMEM((groups, share, FEAT_PAD), BF16),
                pltpu.VMEM((groups // 2, share, FEAT_PAD), BF16),
                pltpu.VMEM((mine, share, FEAT_PAD), F32),
                pltpu.VMEM((mine, share, FEAT_PAD), BF16),
                pltpu.VMEM((mine, share, FEAT_PAD), BF16),
                pltpu.VMEM((mine, share, FEAT_PAD), BF16),
                pltpu.VMEM((outer, share, FEAT_PAD), BF16),
                pltpu.VMEM((share, FEAT_PAD), BF16),
                pltpu.VMEM((chips, share, SPAN), BF16),
                pltpu.VMEM((8, 128), F32),
                pltpu.VMEM((members, 8, 128), F32),
                pltpu.VMEM((8, 128), F32),
                pltpu.VMEM((groups, 8, 128), F32),
                dma((6,)),
                dma((4, members, PAIRS)),
                dma((4, members, PAIRS)),
                dma((members,)),
                dma((members,)),
                dma((members,)),
                dma((members,)),
                dma((members,)),
                dma((members,)),
                dma((groups,)),
                dma((groups,)),
                dma,
                dma,
                dma((mine,)),
                dma((mine,)),
                dma((mine,)),
                dma((outer,)),
                dma((members,)),
                dma((chips,)),
            ],
            compiler_params=pltpu.CompilerParams(collective_id=0, has_side_effects=True, vmem_limit_bytes=65900000),
            name="sublayer",
        )(
            lengths,
            segments,
            query_rows[0].T,
            key_rows[0].T,
            value_rows[0].T,
            out_weight,
            target[0],
        )
        final = pl.pallas_call(
            functools.partial(scale_kernel, groups * total, total),
            out_shape=(
                jax.ShapeDtypeStruct((FEAT, rows), F32),
                jax.ShapeDtypeStruct((FEAT, rows), F32),
                jax.ShapeDtypeStruct((FEAT, rows), F32),
                jax.ShapeDtypeStruct((FEAT // members, share), F32),
                jax.ShapeDtypeStruct((1, 1), F32),
            ),
            in_specs=[vmem] * 5,
            out_specs=(vmem,) * 5,
            compiler_params=pltpu.CompilerParams(vmem_limit_bytes=65900000),
            name="scale",
        )(outs[4], *outs[:4])
        return (final[0].T[None], final[1].T[None], final[2].T[None], final[3], final[4].reshape(()))

    placed = (
        P("dp", "patch", None),
        P("dp", "patch", None),
        P("dp", "patch", None),
        P(),
        P("dp", "patch", None),
        P("dp"),
        P("dp", "patch"),
    )
    return jax.shard_map(
        local,
        mesh=mesh,
        in_specs=placed,
        out_specs=(
            P("dp", "patch", None),
            P("dp", "patch", None),
            P("dp", "patch", None),
            P("patch", "dp"),
            P(),
        ),
        check_vma=False,
    )
```

time: 58.6 us -> 44.7 us (0.76)
  local copies, waits for them, and re-layouts: 11.6 us -> 0 us
  Pallas kernels: 45.4 us -> 43.3 us
    unnamed x11 -> x0, local copies, waits for them, and re-layouts: 10.3 us -> none
    pallas_call x1, Pallas kernels: 45.4 us -> 41 us  [local(): pl.pallas_call(functools.partial(kernel, members, groups), out_shape=(jax...]
    pallas_call x0 -> x1, Pallas kernels: none -> 2.27 us  [local(): pl.pallas_call(functools.partial(scale_kernel, groups * total, total), ou...]
    slice x1 -> x0, local copies, waits for them, and re-layouts: 1.24 us -> none  [local(): return (outs[0][None], outs[1][None], outs[2][None], outs[3], outs[4][0, 0])]
where the time goes in v2:
time: 44.7 us; the launch traced here: 44.6 us
  Pallas kernels  43.3 us (97%)
  between operations  1.29 us (3%)
    pallas_call x1, Pallas kernels, local(): pl.pallas_call(functools.partial(kernel, members, groups), out_shape=(jax...  41 us
    pallas_call x1, Pallas kernels, local(): pl.pallas_call(functools.partial(scale_kernel, groups * total, total), ou...  2.27 us

profile of v2, /device:TPU:9, one launch (start us, length us, event | category | flops | bytes accessed | tf_op | source)
XLA Modules:
  0.0 44.6 jit_solution(8245681412899313144)
XLA Ops:
  1.3 41.0 %sublayer.1 = (f32[576,128]{1,0:T(8,128)}, f32[576,128]{1,0:T(8,128)}, f32[576,128]{1,0:T(8,128)}, f32[144,144]{1,0:T(8,128)}, f32[8,128]{1,0:T(8,128)}) custom-call(s32[1]{0:T(128)S(6)} %copy.12.len_ref, s32[1,128]{1,0:T(1,128)} %seg_ref.1, bf16[576,128]{1,0:T(8,128)(2,1)} %bitcast.21, bf16[576,128]{1,0:T(8,128)(2,1)} %bitcast.22, ...), custom_call_target="tpu_custom_call" | custom-call | tf_op jit(solution)/shard_map/sublayer/pallas_call | solution.py:461
  42.3 2.3 %scale.1 = (f32[576,128]{1,0:T(8,128)}, f32[576,128]{1,0:T(8,128)}, f32[576,128]{1,0:T(8,128)}, f32[144,144]{1,0:T(8,128)}, f32[1,1]{1,0:T(1,128)}) custom-call(f32[8,128]{1,0:T(8,128)} %get-tuple-element.15.sum_ref, f32[576,128]{1,0:T(8,128)} %get-tuple-element.16.dq_ref, f32[576,128]{1,0:T(8,128)} %get-tuple-element.17.dk_ref, ...), custom_call_target="tpu_custom_call" | custom-call | tf_op jit(solution)/shard_map/scale/pallas_call | solution.py:530

commit v3 on v2

--- a/solution.py
+++ b/solution.py
@@ -297,13 +297,22 @@
         dq_ref[PAIR_ROWS * pair : PAIR_ROWS * (pair + 1), :] = merged(value) * score_scale
 
     stage1.wait_recv()
-    stage2 = []
-    for i in range(mine):
-        away = 2 * i + 1 - step_b
-        wx_ref[i] = (part_ref[first + away].astype(F32) + w1_ref[away].astype(F32)).astype(BF16)
-        item = copy(wx_ref.at[i], w2_ref.at[i], s2.at[i], r2.at[i], (step_a * 2 + 1 - step_b, me))
+    cut = -(-share // 32) * 16
+    pieces = [(i, side) for i in range(mine) for side in (0, 1)]
+    spans = [pl.ds(0, cut), pl.ds(cut, share - cut)]
+    stage2 = {}
+    for i, side in pieces:
+        away, span = 2 * i + 1 - step_b, spans[side]
+        wx_ref[i, span] = (part_ref[first + away, span].astype(F32) + w1_ref[away, span].astype(F32)).astype(BF16)
+        item = copy(
+            wx_ref.at[i, span],
+            w2_ref.at[i, span],
+            s2.at[i, side],
+            r2.at[i, side],
+            (step_a * 2 + 1 - step_b, me),
+        )
         start(item)
-        stage2.append(item)
+        stage2[i, side] = item
     for i in range(mine):
         near = 2 * i + step_b
         keep_ref[i] = part_ref[first + near].astype(F32) + w1_ref[near].astype(F32)
@@ -311,7 +320,6 @@
         relay(QUERY, pair)
 
     query_pass(0)
-    query_pass(1)
     relay(GRAD, 0)
     relay(GRAD, 1)
     small_wait(stat_own, stat_all, stat_send, stat_recv)
@@ -319,11 +327,18 @@
         tall = jnp.concatenate([stat_all[j], jnp.zeros((128 - 2 * HEADS, rows), F32)], axis=0)
         stat_columns[j * rows : (j + 1) * rows, :] = tall.T
 
-    def third(i):
-        stage2[i].wait_recv()
-        wz_ref[i] = (keep_ref[i] + w2_ref[i].astype(F32)).astype(BF16)
+    def third(i, side):
+        span = spans[side]
+        stage2[i, side].wait_recv()
+        wz_ref[i, span] = (keep_ref[i, span] + w2_ref[i, span].astype(F32)).astype(BF16)
         owner = core * mine + i
-        item = copy(wz_ref.at[i], w3_ref.at[step_a], s3.at[i], r3.at[step_a], (owner * 2 + step_b, me))
+        item = copy(
+            wz_ref.at[i, span],
+            w3_ref.at[step_a, span],
+            s3.at[i, side],
+            r3.at[step_a, side],
+            (owner * 2 + step_b, me),
+        )
 
         @pl.when(owner != step_a)
         def _():
@@ -350,12 +365,15 @@
         dscores = (probs * (dprobs - columns(HEADS))).astype(BF16)
         dk_ref[PAIR_ROWS * pair : PAIR_ROWS * (pair + 1), :] = merged(nn(queries, dscores)) * score_scale
 
-    stage3 = [third(0)]
+    stage3 = [third(*pieces[0])]
     relay(GRAD, 2)
     relay(GRAD, 3)
+    query_pass(1)
+    stage3.append(third(*pieces[1]))
     query_pass(2)
-    stage3 += [third(i) for i in range(1, mine)]
+    stage3.append(third(*pieces[2]))
     query_pass(3)
+    stage3 += [third(*piece) for piece in pieces[3:]]
 
     small_wait(tile_own, tile_all, tile_send, tile_recv)
     tile_all[me] = tile_own[...]
@@ -384,7 +402,9 @@
         summed = wz_ref[step_a - core * mine].astype(F32)
         for shift in range(1, outer):
             source = lax.rem(step_a + shift, outer)
-            copy(wz_ref.at[0], w3_ref.at[source], s3.at[0], r3.at[source], (source * 2 + step_b, me)).wait_recv()
+            for side, span in enumerate(spans):
+                slot = w3_ref.at[source, span]
+                copy(slot, slot, s3.at[0, side], r3.at[source, side], (source * 2 + step_b, me)).wait_recv()
             summed = summed + w3_ref[source].astype(F32)
         fin_ref[...] = summed.astype(BF16)
         for item in stage4:
@@ -509,10 +529,10 @@
                 dma((groups,)),
                 dma,
                 dma,
-                dma((mine,)),
-                dma((mine,)),
-                dma((mine,)),
-                dma((outer,)),
+                dma((mine, 2)),
+                dma((mine, 2)),
+                dma((mine, 2)),
+                dma((outer, 2)),
                 dma((members,)),
                 dma((chips,)),
             ],

time: 44.7 us -> 43.4 us (0.971)
  Pallas kernels: 43.3 us -> 41.9 us
    pallas_call x1, Pallas kernels: 41 us -> 39.6 us  [local(): pl.pallas_call(functools.partial(kernel, members, groups), out_shape=(jax...]
where the time goes in v3:
time: 43.4 us; the launch traced here: 43.2 us
  Pallas kernels  41.9 us (97%)
  between operations  1.29 us (3%)
    pallas_call x1, Pallas kernels, local(): pl.pallas_call(functools.partial(kernel, members, groups), out_shape=(jax...  39.6 us
    pallas_call x1, Pallas kernels, local(): pl.pallas_call(functools.partial(scale_kernel, groups * total, total), ou...  2.27 us

profile of v3, /device:TPU:9, one launch (start us, length us, event | category | flops | bytes accessed | tf_op | source)
XLA Modules:
  0.0 43.2 jit_solution(2504933567489998463)
XLA Ops:
  1.3 39.6 %sublayer.1 = (f32[576,128]{1,0:T(8,128)}, f32[576,128]{1,0:T(8,128)}, f32[576,128]{1,0:T(8,128)}, f32[144,144]{1,0:T(8,128)}, f32[8,128]{1,0:T(8,128)}) custom-call(s32[1]{0:T(128)S(6)} %copy.12.len_ref, s32[1,128]{1,0:T(1,128)} %seg_ref.1, bf16[576,128]{1,0:T(8,128)(2,1)} %bitcast.21, bf16[576,128]{1,0:T(8,128)(2,1)} %bitcast.22, ...), custom_call_target="tpu_custom_call" | custom-call | tf_op jit(solution)/shard_map/sublayer/pallas_call | solution.py:481
  40.9 2.3 %scale.1 = (f32[576,128]{1,0:T(8,128)}, f32[576,128]{1,0:T(8,128)}, f32[576,128]{1,0:T(8,128)}, f32[144,144]{1,0:T(8,128)}, f32[1,1]{1,0:T(1,128)}) custom-call(f32[8,128]{1,0:T(8,128)} %get-tuple-element.15.sum_ref, f32[576,128]{1,0:T(8,128)} %get-tuple-element.16.dq_ref, f32[576,128]{1,0:T(8,128)} %get-tuple-element.17.dk_ref, ...), custom_call_target="tpu_custom_call" | custom-call | tf_op jit(solution)/shard_map/scale/pallas_call | solution.py:550
